TPU v7x, 32 devices: a whole 2x2x4 slice. The times are simulated.
32 devices in a mesh: ctx: 8 (over y, x, core), dp: 4 (over z).
Axes of the slice: x: 2, y: 2, z: 4, core: 2. Of those that a mesh axis runs over, the one named last changes fastest.
Arguments:
- query: bfloat16 [4, 1024, 512], P('dp', 'ctx'), may hold values from -6 to 6
- key_input: bfloat16 [4, 1024, 512], P('dp', 'ctx'), may hold values from -6 to 6
- value_input: bfloat16 [4, 1024, 512], P('dp', 'ctx'), may hold values from -6 to 6
- filter_taps: float32 [1024, 512], P('ctx'), may hold values from -6 to 6
- grad_output: bfloat16 [4, 1024, 512], P('dp', 'ctx'), may hold values from -6 to 6
Outputs:
- output: bfloat16 [4, 1024, 512], P('dp', 'ctx')
- grad_query: bfloat16 [4, 1024, 512], P('dp', 'ctx')
- grad_key: bfloat16 [4, 1024, 512], P('dp', 'ctx')
- grad_value: bfloat16 [4, 1024, 512], P('dp', 'ctx')
- grad_filter: float32 [1024, 512], P('ctx')
All inputs are finite; a program needn't handle non-finite values.
Results may differ from a plain program's by a relative error of at most 0.0058.
Values may be sent and summed in bfloat16 or wider, within the bound.
A program may use at most 64 MiB of HBM per device.

v0:
```python
import functools
import math

import jax
import jax.numpy as jnp
import numpy as np
from jax import lax
from jax.experimental import pallas as pl
from jax.experimental.pallas import tpu as pltpu
from jax.sharding import PartitionSpec as P

HIGH = lax.Precision.HIGHEST
MESH = pl.DeviceIdType.MESH
LANES = 128
VMEM_BYTES = 67043328
F32 = jnp.float32
BF16 = jnp.bfloat16


def block_tables(length):
    odd = 2 * np.arange(length, dtype=np.int64)[:, None] + 1
    angle = (odd * np.arange(length, dtype=np.int64)[None, :] % (4 * length)) * (2.0 * math.pi / (4 * length))
    ahead = np.concatenate([np.cos(angle), -np.sin(angle)], axis=0).astype(np.float32)
    back = ahead.T / np.float32(length)

    def split(table):
        high = jnp.asarray(table).astype(BF16)
        low = (jnp.asarray(table) - high.astype(F32)).astype(BF16)
        return high, low

    with jax.ensure_compile_time_eval():
        ahead_high, ahead_low = split(ahead)
        back_high, back_low = split(back)
        return (
            np.asarray(jnp.concatenate([ahead_high, ahead_low], axis=1)),
            np.asarray(jnp.concatenate([back_high, back_low], axis=1)),
        )


def merge(first, second, low):
    half = first.shape[-1] // 2
    turned = pltpu.roll(jnp.where(low, second, first), half, 1)
    return jnp.where(low, first, turned), jnp.where(low, turned, second)


def kernel(
    nctx,
    ndp,
    q_hbm,
    k_hbm,
    v_hbm,
    f_hbm,
    g_hbm,
    ahead_hbm,
    back_hbm,
    mg_rx,
    g2_rx,
    qv,
    kv,
    vv,
    gv,
    fv,
    ahead_v,
    back_v,
    send1,
    rx1,
    sendf,
    rxf,
    sig,
    wei,
    oth,
    gfs,
    rs_send,
    rs_rx,
    g2_send,
    mg_send,
    known,
    load_sem,
    s1_send,
    s1_recv,
    sf_send,
    sf_recv,
    rs_ssem,
    rs_rsem,
    g2_ssem,
    g2_rsem,
    mg_ssem,
    mg_rsem,
):
    me = lax.axis_index("ctx")
    row = lax.axis_index("dp")
    length = qv.shape[1]
    hl = length // 2
    tiles = nctx // 2

    pairs = ((k_hbm, kv), (v_hbm, vv), (g_hbm, gv), (q_hbm, qv), (f_hbm, fv), (ahead_hbm, ahead_v), (back_hbm, back_v))
    loads = [pltpu.make_async_copy(src, dst, load_sem.at[n]) for n, (src, dst) in enumerate(pairs)]
    for load in loads:
        load.start()

    barrier = pltpu.get_barrier_semaphore()
    for oc in range(1, nctx):
        pl.semaphore_signal(
            barrier, inc=1, device_id={"ctx": lax.rem(me + oc, nctx), "dp": row}, device_id_type=MESH
        )
    for step, there in ((1, row + 1 < ndp), (-1, row > 0)):

        @pl.when(there)
        def _(step=step):
            pl.semaphore_signal(barrier, inc=1, device_id={"ctx": me, "dp": row + step}, device_id_type=MESH)

    low = lax.broadcasted_iota(jnp.int32, (length, LANES), 1) < LANES // 2
    low_h = lax.broadcasted_iota(jnp.int32, (hl, LANES), 1) < LANES // 2
    for load in loads[:4]:
        load.wait()
    for p in range(tiles):
        cols = slice(p * LANES, (p + 1) * LANES)
        x = (kv[0, :, cols].astype(F32) * vv[0, :, cols].astype(F32)).astype(BF16).astype(F32)
        g = (gv[0, :, cols].astype(F32) * qv[0, :, cols].astype(F32)).astype(BF16).astype(F32)
        even, odd = merge(x, g, low)
        send1[2 * p] = even.astype(BF16)
        send1[2 * p + 1] = odd.astype(BF16)

    beside = jnp.where(row + 1 < ndp, 1, 0) + jnp.where(row > 0, 1, 0)
    pl.semaphore_wait(barrier, nctx - 1 + beside)

    def copy1(peer, slot):
        return pltpu.make_async_remote_copy(
            src_ref=send1.at[peer],
            dst_ref=rx1.at[slot],
            send_sem=s1_send.at[peer],
            recv_sem=s1_recv.at[slot],
            device_id={"ctx": peer, "dp": row},
            device_id_type=MESH,
        )

    def copyf(peer, slot):
        return pltpu.make_async_remote_copy(
            src_ref=sendf.at[peer],
            dst_ref=rxf.at[slot],
            send_sem=sf_send.at[peer],
            recv_sem=sf_recv.at[slot],
            device_id={"ctx": peer, "dp": row},
            device_id_type=MESH,
        )

    order = [nctx // 2 + o for o in range(nctx // 2)] + list(range(1, nctx // 2))
    peers = [lax.rem(me + o, nctx) for o in order]
    for peer in peers:
        copy1(peer, me).start()
    for n, (step, dist) in enumerate(((1, row), (-1, ndp - 1 - row))):

        @pl.when(dist >= 2)
        def _(n=n):
            pl.semaphore_wait(known.at[n], 1)

        @pl.when(jnp.logical_and(dist >= 1, dist + 1 < ndp))
        def _(n=n, step=step):
            pl.semaphore_signal(
                known.at[n], inc=1, device_id={"ctx": me, "dp": row + step}, device_id_type=MESH
            )

    loads[4].wait()
    for p in range(tiles):
        cols = slice(p * LANES, (p + 1) * LANES)
        even, odd = merge(fv[0:hl, cols], fv[hl:length, cols], low_h)
        sendf[2 * p] = even.astype(BF16)
        sendf[2 * p + 1] = odd.astype(BF16)
    for load in loads[5:]:
        load.wait()
    for peer in peers:
        copyf(peer, me).start()

    def transform(z):
        return jnp.dot(ahead_v[...], jnp.concatenate([z, z], axis=0), preferred_element_type=F32)

    def weigh(fa):
        fa = fa.astype(F32)
        turned = pltpu.roll(fa, LANES // 2, 1)
        w = jnp.concatenate([jnp.where(low_h, fa, turned), jnp.where(low_h, turned, fa)], axis=0)
        return transform(w.astype(BF16))

    sig[me] = transform(send1[me])
    for peer in reversed(peers):
        copy1(peer, peer).wait_recv()
        sig[peer] = transform(rx1[peer])

    lane8 = lax.broadcasted_iota(jnp.int32, (8, LANES), 1) < LANES // 2
    parity = lax.rem(lax.broadcasted_iota(jnp.int32, (8, LANES), 0), 2)
    alt = jnp.where(parity == 0, 1.0, -1.0).astype(F32)
    lane_sign = jnp.where(lane8, 1.0, -1.0).astype(F32)
    both_sign = alt * lane_sign

    @pl.loop(0, length // 8)
    def _(i):
        re = pl.ds(pl.multiple_of(i * 8, 8), 8)
        im = pl.ds(pl.multiple_of(length + i * 8, 8), 8)
        s_re = [sig[d, re, :] for d in range(nctx)]
        s_im = [sig[d, im, :] for d in range(nctx)]
        u_re = [jnp.where(lane8, pltpu.roll(a, LANES // 2, 1), a) for a in s_re]
        u_im = [jnp.where(lane8, pltpu.roll(a, LANES // 2, 1), a) for a in s_im]
        x_re = [s_re[0]] + [s_re[n] - alt * s_im[n - 1] for n in range(1, nctx)]
        x_im = [s_im[0]] + [s_im[n] + alt * s_re[n - 1] for n in range(1, nctx)]
        v_re = [jnp.where(lane8, x_re[n], 0.0) for n in range(tiles)]
        v_im = [jnp.where(lane8, x_im[n], 0.0) for n in range(tiles)]
        for n in range(tiles, nctx):
            v_re.append(jnp.where(lane8, x_re[n], pltpu.roll(x_re[n - tiles], LANES // 2, 1)))
            v_im.append(jnp.where(lane8, x_im[n], pltpu.roll(x_im[n - tiles], LANES // 2, 1)))
        for j in range(tiles):
            a_re = jnp.zeros((8, LANES), F32)
            a_im = jnp.zeros((8, LANES), F32)
            for m in range(j, nctx):
                n = m - j
                a_re = a_re + u_re[m] * v_re[n] + u_im[m] * v_im[n]
                a_im = a_im + u_im[m] * v_re[n] - u_re[m] * v_im[n]
            gfs[j, re, :] = a_re
            gfs[j, im, :] = a_im

    def inverse(spec):
        high = spec.astype(BF16)
        return jnp.dot(back_v[...], jnp.concatenate([high, high], axis=0), preferred_element_type=F32)

    def copy_rs(peer, slot):
        return pltpu.make_async_remote_copy(
            src_ref=rs_send.at[peer],
            dst_ref=rs_rx.at[slot],
            send_sem=rs_ssem.at[peer],
            recv_sem=rs_rsem.at[slot],
            device_id={"ctx": me, "dp": peer},
            device_id_type=MESH,
        )

    for j in range(tiles):
        rs_send[j] = inverse(gfs[j]).astype(BF16)
    rows_peers = [lax.rem(row + o, ndp) for o in range(1, ndp)]
    for peer in rows_peers:
        copy_rs(peer, row).start()

    wei[me] = weigh(sendf[me])
    for peer in reversed(peers):
        copyf(peer, peer).wait_recv()
        wei[peer] = weigh(rxf[peer])

    @pl.loop(0, length // 8)
    def _(i):
        re = pl.ds(pl.multiple_of(i * 8, 8), 8)
        im = pl.ds(pl.multiple_of(length + i * 8, 8), 8)
        s_re = [sig[d, re, :] for d in range(nctx)]
        s_im = [sig[d, im, :] for d in range(nctx)]
        q_re = [jnp.where(lane8, s_re[n], s_re[nctx - 1 - n]) for n in range(nctx)]
        q_im = [jnp.where(lane8, s_im[n], s_im[nctx - 1 - n]) for n in range(nctx)]
        z_re = [q_re[0]] + [q_re[n] - both_sign * q_im[n - 1] for n in range(1, nctx)]
        z_im = [q_im[0]] + [q_im[n] + both_sign * q_re[n - 1] for n in range(1, nctx)]
        w_re = [wei[d, re, :] for d in range(nctx)]
        w_im = [wei[d, im, :] * lane_sign for d in range(nctx)]
        o_re, o_im = [], []
        for n in range(nctx):
            a_re = jnp.zeros((8, LANES), F32)
            a_im = jnp.zeros((8, LANES), F32)
            for j in range(n + 1):
                a_re = a_re + w_re[j] * z_re[n - j] - w_im[j] * z_im[n - j]
                a_im = a_im + w_re[j] * z_im[n - j] + w_im[j] * z_re[n - j]
            o_re.append(a_re)
            o_im.append(a_im)
        for d in range(nctx):
            oth[d, re, :] = jnp.where(lane8, o_re[d], o_re[nctx - 1 - d])
            oth[d, im, :] = jnp.where(lane8, o_im[d], o_im[nctx - 1 - d])

    def copy_mg(peer, slot):
        return pltpu.make_async_remote_copy(
            src_ref=mg_send.at[peer],
            dst_ref=mg_rx.at[slot],
            send_sem=mg_ssem.at[peer],
            recv_sem=mg_rsem.at[slot],
            device_id={"ctx": peer, "dp": row},
            device_id_type=MESH,
        )

    for at, peer in enumerate(peers):
        mg_send[peer] = inverse(oth[peer]).astype(BF16)
        if at:
            copy_mg(peers[at - 1], me).start()
    mg_rx[me] = inverse(oth[me]).astype(BF16)
    copy_mg(peers[-1], me).start()

    total = rs_send[row].astype(F32)
    for peer in rows_peers:
        copy_rs(peer, peer).wait_recv()
        total = total + rs_rx[peer].astype(F32)
    first, second = merge(total[0:hl], total[hl:length], low_h)
    g2_send[0] = first.astype(BF16)
    g2_send[1] = second.astype(BF16)

    def copy_g2(part, to_row, slot):
        return pltpu.make_async_remote_copy(
            src_ref=g2_send.at[part],
            dst_ref=g2_rx.at[slot],
            send_sem=g2_ssem.at[part, to_row],
            recv_sem=g2_rsem.at[slot],
            device_id={"ctx": row + part * tiles, "dp": to_row},
            device_id_type=MESH,
        )

    for part in range(2):
        for o in range(1, ndp):
            copy_g2(part, lax.rem(row + o, ndp), me).start()
        mine = me == row + part * tiles

        @pl.when(mine)
        def _():
            g2_rx[me] = g2_send[part]

        @pl.when(jnp.logical_not(mine))
        def _():
            copy_g2(part, row, me).start()

    for peer in peers:
        copy_mg(peer, peer).wait_recv()

    from_row = lax.rem(me, tiles)
    for c in range(nctx):
        outside = jnp.logical_not(jnp.logical_and(me == c, row == from_row))

        @pl.when(outside)
        def _():
            copy_g2(0, row, c).wait_recv()

    for peer in peers:
        copy1(peer, me).wait_send()
        copyf(peer, me).wait_send()
        copy_mg(peer, me).wait_send()
    for peer in rows_peers:
        copy_rs(peer, row).wait_send()
    for part in range(2):
        for o in range(1, ndp):
            copy_g2(part, lax.rem(row + o, ndp), me).wait_send()

        @pl.when(jnp.logical_not(me == row + part * tiles))
        def _():
            copy_g2(part, row, me).wait_send()


def finish(mg, g2, q, k, v, g, out_hbm, gq_hbm, gk_hbm, gv_hbm, gf_hbm, out_v, gq_v, gk_v, gv_v, gf_v, sems):
    length = q.shape[1]
    hl = length // 2
    tiles = mg.shape[0] // 2
    low = lax.broadcasted_iota(jnp.int32, (length, LANES), 1) < LANES // 2
    low_h = lax.broadcasted_iota(jnp.int32, (hl, LANES), 1) < LANES // 2
    copies = []

    def put(n, p, src, dst):
        copy = pltpu.make_async_copy(src, dst, sems.at[n, p])
        copy.start()
        copies.append(copy)

    for p in range(tiles):
        cols = slice(p * LANES, (p + 1) * LANES)
        mixed, back = merge(mg[2 * p].astype(F32), mg[2 * p + 1].astype(F32), low)
        out_v[0, :, cols] = (q[0, :, cols].astype(F32) * mixed).astype(BF16)
        gq_v[0, :, cols] = (g[0, :, cols].astype(F32) * mixed).astype(BF16)
        gk_v[0, :, cols] = (v[0, :, cols].astype(F32) * back).astype(BF16)
        gv_v[0, :, cols] = (k[0, :, cols].astype(F32) * back).astype(BF16)
        top, bottom = merge(g2[2 * p].astype(F32), g2[2 * p + 1].astype(F32), low_h)
        gf_v[0:hl, cols] = top
        gf_v[hl:length, cols] = bottom
        for n, (src, dst) in enumerate(((out_v, out_hbm), (gq_v, gq_hbm), (gk_v, gk_hbm), (gv_v, gv_hbm))):
            put(n, p, src.at[:, :, cols], dst.at[:, :, cols])
        put(4, p, gf_v.at[:, cols], gf_hbm.at[:, cols])
    for copy in copies:
        copy.wait()


def fused(nctx, ndp, query, key_input, value_input, filter_taps, grad_output):
    length, channels = query.shape[1], query.shape[2]
    ahead, back = block_tables(length)
    vm = pl.BlockSpec(memory_space=pltpu.VMEM)
    hbm = pl.BlockSpec(memory_space=pltpu.HBM)
    hl, tiles = length // 2, nctx // 2
    dma = pltpu.SemaphoreType.DMA
    kept = 2 * (4 * query.size + nctx * (length + hl) * LANES) + 16384
    arrived = pl.pallas_call(
        functools.partial(kernel, nctx, ndp),
        out_shape=(
            pltpu.VMEM((nctx, length, LANES), BF16),
            pltpu.VMEM((nctx, hl, LANES), BF16),
            pltpu.VMEM(query.shape, BF16),
            pltpu.VMEM(query.shape, BF16),
            pltpu.VMEM(query.shape, BF16),
            pltpu.VMEM(query.shape, BF16),
        ),
        in_specs=[hbm] * 7,
        out_specs=(vm,) * 6,
        scratch_shapes=[
            pltpu.VMEM((length, channels), F32),
            pltpu.VMEM(ahead.shape, BF16),
            pltpu.VMEM(back.shape, BF16),
            pltpu.VMEM((nctx, length, LANES), BF16),
            pltpu.VMEM((nctx, length, LANES), BF16),
            pltpu.VMEM((nctx, hl, LANES), BF16),
            pltpu.VMEM((nctx, hl, LANES), BF16),
            pltpu.VMEM((nctx, 2 * length, LANES), F32),
            pltpu.VMEM((nctx, 2 * length, LANES), F32),
            pltpu.VMEM((nctx, 2 * length, LANES), F32),
            pltpu.VMEM((tiles, 2 * length, LANES), F32),
            pltpu.VMEM((tiles, length, LANES), BF16),
            pltpu.VMEM((ndp, length, LANES), BF16),
            pltpu.VMEM((2, hl, LANES), BF16),
            pltpu.VMEM((nctx, length, LANES), BF16),
            pltpu.SemaphoreType.REGULAR((2,)),
            dma((7,)),
            dma((nctx,)),
            dma((nctx,)),
            dma((nctx,)),
            dma((nctx,)),
            dma((ndp,)),
            dma((ndp,)),
            dma((2, ndp)),
            dma((nctx,)),
            dma((nctx,)),
            dma((nctx,)),
        ],
        compiler_params=pltpu.CompilerParams(
            collective_id=0, has_side_effects=True, vmem_limit_bytes=VMEM_BYTES - kept
        ),
    )(query, key_input, value_input, filter_taps, grad_output, jnp.asarray(ahead), jnp.asarray(back))
    wide = jax.ShapeDtypeStruct(query.shape, BF16)
    return pl.pallas_call(
        finish,
        out_shape=(wide, wide, wide, wide, jax.ShapeDtypeStruct((length, channels), F32)),
        in_specs=[vm] * 6,
        out_specs=(hbm,) * 5,
        scratch_shapes=[pltpu.VMEM(query.shape, BF16)] * 4 + [pltpu.VMEM((length, channels), F32), dma((5, tiles))],
        compiler_params=pltpu.CompilerParams(vmem_limit_bytes=16 * 1024 * 1024),
    )(*arrived)


def build_tables(length):
    padded = 2 * length
    columns = 1
    while columns * columns < padded and length % (2 * columns) == 0:
        columns = columns * 2
    row_count = padded // columns
    col_index = jnp.arange(columns, dtype=jnp.int32)
    row_index = jnp.arange(row_count, dtype=jnp.int32)
    col_angle = (col_index[:, None] * col_index[None, :] % columns).astype(jnp.float32) * (
        2.0 * math.pi / columns
    )
    row_angle = (row_index[:, None] * row_index[None, :] % row_count).astype(jnp.float32) * (
        2.0 * math.pi / row_count
    )
    twist_angle = (row_index[:, None] * col_index[None, :] % padded).astype(jnp.float32) * (
        2.0 * math.pi / padded
    )
    return (
        jnp.cos(col_angle),
        -jnp.sin(col_angle),
        jnp.cos(row_angle),
        -jnp.sin(row_angle),
        jnp.cos(twist_angle),
        -jnp.sin(twist_angle),
        row_count,
        columns,
        padded,
    )


def forward(signal, tables):
    col_real, col_imag, row_real, row_imag, twist_real, twist_imag, row_count, columns, padded = (
        tables
    )
    half_rows = row_count // 2
    blocks = signal.reshape(signal.shape[0], half_rows, columns, signal.shape[2])
    section_real = jnp.einsum("kn,snac->scka", row_real[:, :half_rows], blocks, precision=HIGH)
    section_imag = jnp.einsum("kn,snac->scka", row_imag[:, :half_rows], blocks, precision=HIGH)
    turned_real = section_real * twist_real - section_imag * twist_imag
    turned_imag = section_real * twist_imag + section_imag * twist_real
    spec_real = jnp.einsum("scka,aj->sckj", turned_real, col_real, precision=HIGH) - jnp.einsum(
        "scka,aj->sckj", turned_imag, col_imag, precision=HIGH
    )
    spec_imag = jnp.einsum("scka,aj->sckj", turned_real, col_imag, precision=HIGH) + jnp.einsum(
        "scka,aj->sckj", turned_imag, col_real, precision=HIGH
    )
    return (spec_real, spec_imag)


def inverse(spec, tables):
    col_real, col_imag, row_real, row_imag, twist_real, twist_imag, row_count, columns, padded = (
        tables
    )
    spec_real, spec_imag = spec
    half_rows = row_count // 2
    section_real = jnp.einsum("scka,aj->sckj", spec_real, col_real, precision=HIGH) + jnp.einsum(
        "scka,aj->sckj", spec_imag, col_imag, precision=HIGH
    )
    section_imag = jnp.einsum("scka,aj->sckj", spec_imag, col_real, precision=HIGH) - jnp.einsum(
        "scka,aj->sckj", spec_real, col_imag, precision=HIGH
    )
    turned_real = section_real * twist_real + section_imag * twist_imag
    turned_imag = section_imag * twist_real - section_real * twist_imag
    signal = jnp.einsum(
        "nk,scka->snac", row_real[:half_rows], turned_real, precision=HIGH
    ) + jnp.einsum("nk,scka->snac", row_imag[:half_rows], turned_imag, precision=HIGH)
    return signal.reshape(signal.shape[0], half_rows * columns, signal.shape[3]) * (1.0 / padded)


def times_spec(first, second):
    return (
        first[0] * second[0] - first[1] * second[1],
        first[0] * second[1] + first[1] * second[0],
    )


def times_conj(first, second):
    return (
        first[0] * second[0] + first[1] * second[1],
        first[1] * second[0] - first[0] * second[1],
    )


def local(query, key_input, value_input, filter_taps, grad_output):
    product = (key_input.astype(jnp.float32) * value_input.astype(jnp.float32)).astype(jnp.bfloat16)
    grad_mix = (grad_output.astype(jnp.float32) * query.astype(jnp.float32)).astype(jnp.bfloat16)
    owned_filter = lax.all_to_all(filter_taps, "ctx", split_axis=1, concat_axis=0, tiled=True)
    tables = build_tables(owned_filter.shape[0])
    filter_spec = forward(owned_filter[None], tables)
    local_product = lax.all_to_all(product, "ctx", split_axis=2, concat_axis=1, tiled=True)
    prod_spec = forward(local_product.astype(jnp.float32), tables)
    owned_mixed = inverse(times_spec(filter_spec, prod_spec), tables).astype(jnp.bfloat16)
    owned_mixed, prod_spec = (owned_mixed, prod_spec)
    mixed = lax.all_to_all(owned_mixed, "ctx", split_axis=1, concat_axis=2, tiled=True)
    owned_grad = lax.all_to_all(grad_mix, "ctx", split_axis=2, concat_axis=1, tiled=True)
    grad_spec = forward(owned_grad.astype(jnp.float32), tables)
    owned_back = inverse(times_conj(grad_spec, filter_spec), tables).astype(jnp.bfloat16)
    taps_spec = times_conj(grad_spec, prod_spec)
    owned_back, taps_spec = (
        owned_back,
        (jnp.sum(taps_spec[0], axis=0), jnp.sum(taps_spec[1], axis=0)),
    )
    grad_product = lax.all_to_all(owned_back, "ctx", split_axis=1, concat_axis=2, tiled=True)
    mixed_wide = mixed.astype(jnp.float32)
    back_wide = grad_product.astype(jnp.float32)
    output = (query.astype(jnp.float32) * mixed_wide).astype(jnp.bfloat16)
    grad_query = (grad_output.astype(jnp.float32) * mixed_wide).astype(jnp.bfloat16)
    grad_key = (back_wide * value_input.astype(jnp.float32)).astype(jnp.bfloat16)
    grad_value = (back_wide * key_input.astype(jnp.float32)).astype(jnp.bfloat16)
    local_taps = inverse((taps_spec[0][None], taps_spec[1][None]), tables)[0]
    owned_taps = lax.psum(local_taps, "dp")
    grad_filter = lax.all_to_all(owned_taps, "ctx", split_axis=0, concat_axis=1, tiled=True)
    return (output, grad_query, grad_key, grad_value, grad_filter)


def plan(mesh, query, key_input, value_input, filter_taps, grad_output):
    nctx, ndp = mesh.shape["ctx"], mesh.shape["dp"]
    sequences, length, channels = query.shape
    fits = 2 * channels == nctx * LANES and nctx == 2 * ndp and sequences == 1 and length % 32 == 0 and length <= LANES
    run = functools.partial(fused, nctx, ndp) if fits else local
    return run(query, key_input, value_input, filter_taps, grad_output)


def solution(mesh):
    wide, taps = P("dp", "ctx", None), P("ctx", None)
    return jax.shard_map(
        functools.partial(plan, mesh),
        mesh=mesh,
        in_specs=(wide, wide, wide, taps, wide),
        out_specs=(wide, wide, wide, wide, taps),
        check_vma=False,
    )
```

profile of v0, /device:TPU:0, one launch (start us, length us, event | category | flops | bytes accessed | tf_op | source)
XLA Modules:
  0.0 23.9 jit_solution(297461913432135934)
XLA Ops:
  0.6 22.2 %shard_map.110 = (bf16[8,128,128]{2,1,0:T(8,128)(2,1)S(1)}, bf16[8,64,128]{2,1,0:T(8,128)(2,1)S(1)}, bf16[1,128,512]{2,1,0:T(8,128)(2,1)S(1)}, bf16[1,128,512]{2...) custom-call(bf16[1,128,512]{2,1,0:T(8,128)(2,1)} %q_hbm.1, ...), custom_call_target="tpu_custom_call" | custom-call | tf_op jit(solution)/shard_map/pallas_call | solution.py:381
  22.8 1.2 %shard_map.111 = (bf16[1,128,512]{2,1,0:T(8,128)(2,1)}, bf16[1,128,512]{2,1,0:T(8,128)(2,1)}, bf16[1,128,512]{2,1,0:T(8,128)(2,1)}, bf16[1,128,512]{2,1,0:T(8,128)(2,1)}, f32[128,512]{1,0:T(8,128)}) custom-call(bf16[8,128,128]{2,1,0:T(8,128)(2,1)S(1)} %get-tuple-element.11.mg, bf16[8,64,128]{2,1,0:T(8,128)(2,1)S(1)} %get-tuple-element.12.g2, ...), custom_call_target="tpu_custom_call" | custom-call | tf_op jit(solution)/shard_map/pallas_call | solution.py:427
where the time goes:
time: 24.1 us; the launch traced here: 23.9 us
  Pallas kernels  23.3 us (97%)
  between operations  0.64 us (3%)
    pallas_call x1, Pallas kernels, fused(): pl.pallas_call(functools.partial(kernel, nctx, ndp), out_shape=(pltpu.VME...  22.2 us
    pallas_call x1, Pallas kernels, fused(): pl.pallas_call(finish, out_shape=(wide, wide, wide, wide, jax.ShapeDtypeS...  1.15 us

commit v1 on v0

v1 whole, which is shorter than its diff:
```python
import functools
import math

import jax
import jax.numpy as jnp
import numpy as np
from jax import lax
from jax.experimental import pallas as pl
from jax.experimental.pallas import tpu as pltpu
from jax.sharding import PartitionSpec as P

HIGH = lax.Precision.HIGHEST
MESH = pl.DeviceIdType.MESH
LANES = 128
VMEM_BYTES = 67043328
F32 = jnp.float32
BF16 = jnp.bfloat16


def block_tables(length):
    odd = 2 * np.arange(length, dtype=np.int64)[:, None] + 1
    angle = (odd * np.arange(length, dtype=np.int64)[None, :] % (4 * length)) * (2.0 * math.pi / (4 * length))
    ahead = np.concatenate([np.cos(angle), -np.sin(angle)], axis=0).astype(np.float32)
    back = ahead.T / np.float32(length)

    def split(table):
        high = jnp.asarray(table).astype(BF16)
        low = (jnp.asarray(table) - high.astype(F32)).astype(BF16)
        return high, low

    with jax.ensure_compile_time_eval():
        ahead_high, ahead_low = split(ahead)
        back_high, back_low = split(back)
        return (
            np.asarray(jnp.concatenate([ahead_high, ahead_low], axis=1)),
            np.asarray(jnp.concatenate([back_high, back_low], axis=1)),
        )


def groups(rows, dtype):
    kind = jnp.int16 if dtype == BF16 else jnp.int32
    lane = lax.broadcasted_iota(kind, (rows, LANES), 1)
    low = lane < LANES // 2
    even = (lane < LANES // 4) | ((lane >= LANES // 2) & (lane < 3 * LANES // 4))
    return low, even


def turn(a, b, c, d, masks):
    low, even = masks

    def halves(first, second):
        turned = pltpu.roll(jnp.where(low, second, first), LANES // 2, 1)
        return jnp.where(low, first, turned), jnp.where(low, turned, second)

    def quarters(first, second):
        return (
            jnp.where(even, first, pltpu.roll(second, LANES // 4, 1)),
            jnp.where(even, pltpu.roll(first, LANES - LANES // 4, 1), second),
        )

    (a, c), (b, d) = halves(a, c), halves(b, d)
    return quarters(a, b) + quarters(c, d)


def turn_rows(tile, masks):
    rows = tile.shape[0] // 4
    return turn(*[tile[n * rows : (n + 1) * rows] for n in range(4)], masks)


def flip(index, mask):
    out, bit = index, 1
    while bit <= mask:
        if mask & bit:
            out = out + bit * (1 - 2 * lax.rem(index // bit, 2))
        bit = 2 * bit
    return out


def total(terms):
    out = None
    for term in terms:
        out = term if out is None else out + term
    return out


def kernel(
    nctx,
    ndp,
    q_hbm,
    k_hbm,
    v_hbm,
    f_hbm,
    g_hbm,
    ahead_hbm,
    back_hbm,
    mx_rx,
    mg_rx,
    g2_rx,
    qv,
    kv,
    vv,
    gv,
    fv,
    ahead_v,
    back_v,
    sendx,
    sendg,
    sendf,
    rxx,
    rxg,
    rxf,
    sigx,
    sigg,
    rigx,
    rigg,
    wei,
    othx,
    othg,
    acc,
    gfs,
    g2_send,
    mx_send,
    mg_send,
    known,
    load_sem,
    x_ssem,
    x_rsem,
    g_ssem,
    g_rsem,
    f_ssem,
    f_rsem,
    g2_ssem,
    g2_rsem,
    mx_ssem,
    mx_rsem,
    mg_ssem,
    mg_rsem,
):
    me = lax.axis_index("ctx")
    row = lax.axis_index("dp")
    length = qv.shape[1]
    ql = length // 4
    tiles = nctx // 2
    part = lax.rem(row, 2)
    base = row - part
    other = base + 1 - part
    mine = 2 * me + part
    slot = (row // 2) * 2 * nctx + mine

    pairs = ((k_hbm, kv), (v_hbm, vv), (g_hbm, gv), (q_hbm, qv), (f_hbm, fv), (ahead_hbm, ahead_v), (back_hbm, back_v))
    loads = [pltpu.make_async_copy(src, dst, load_sem.at[n]) for n, (src, dst) in enumerate(pairs)]
    for load in loads:
        load.start()

    def at(ctx, dp):
        return {"ctx": ctx, "dp": dp}

    inner = jnp.logical_and(part == 1, row + 1 < ndp)
    outer = jnp.logical_and(part == 0, row > 0)
    across = row + 2 * part - 1
    border = jnp.logical_or(inner, outer)
    barrier = pltpu.get_barrier_semaphore()
    pals = [(other, me)] + [(r, flip(me, o)) for o in range(1, nctx) for r in (row, other)]
    for r, c in pals:
        pl.semaphore_signal(barrier, inc=1, device_id=at(c, r), device_id_type=MESH)

    @pl.when(border)
    def _():
        pl.semaphore_signal(barrier, inc=1, device_id=at(me, across), device_id_type=MESH)

    masks_q = groups(ql, BF16)

    def prepare(a_ref, b_ref, into):
        for p in range(tiles):
            cols = slice(p * LANES, (p + 1) * LANES)
            tile = (a_ref[0, :, cols].astype(F32) * b_ref[0, :, cols].astype(F32)).astype(BF16)
            for n, piece in enumerate(turn_rows(tile, masks_q)):
                into[4 * p + n] = piece

    for load in loads[:2]:
        load.wait()
    prepare(kv, vv, sendx)
    rxx[mine] = sendx[mine]
    pl.semaphore_wait(barrier, len(pals) + jnp.where(border, 1, 0))

    def remote(src, dst, ssem, rsem, ctx, dp):
        return pltpu.make_async_remote_copy(
            src_ref=src, dst_ref=dst, send_sem=ssem, recv_sem=rsem, device_id=at(ctx, dp), device_id_type=MESH
        )

    def tile_copy(src, dst, ssem, rsem):
        def copy(ctx, dp, into):
            to = 2 * ctx + lax.rem(dp, 2)
            return remote(src.at[to], dst.at[into], ssem, rsem, ctx, dp)

        def whole():
            every = pl.ds(0, len(pals))
            return remote(src.at[every], dst.at[every], ssem, rsem, me, other)

        return copy, whole

    copy_x, all_x = tile_copy(sendx, rxx, x_ssem, x_rsem)
    copy_g, all_g = tile_copy(sendg, rxg, g_ssem, g_rsem)
    copy_mx, all_mx = tile_copy(mx_send, mx_rx, mx_ssem, mx_rsem)
    copy_mg, all_mg = tile_copy(mg_send, mg_rx, mg_ssem, mg_rsem)

    def copy_f(ctx, into):
        return remote(sendf.at[2 * ctx + part], rxf.at[into], f_ssem, f_rsem, ctx, row)

    def copy_g2(ctx, dp, into):
        return remote(g2_send.at[ctx], g2_rx.at[into], g2_ssem, g2_rsem, ctx, dp)

    def all_f():
        every = pl.ds(0, nctx - 1)
        return remote(sendf.at[every], rxf.at[every], f_ssem, f_rsem, me, other)

    def all_g2():
        every = pl.ds(0, nctx * ndp - 1)
        return remote(g2_rx.at[every], g2_rx.at[every], g2_ssem, g2_rsem, me, other)

    for r, c in pals:
        copy_x(c, r, mine).start()

    @pl.when(border)
    def _():
        pl.semaphore_signal(known, inc=1, device_id=at(me, across), device_id_type=MESH)

    others = [k + jnp.where(me <= k, 1, 0) for k in range(nctx - 1)]
    rows_away = [k + jnp.where(row <= k, 1, 0) for k in range(ndp - 1)]

    def spread_grads():
        for load in loads[2:4]:
            load.wait()
        prepare(gv, qv, sendg)
        rxg[mine] = sendg[mine]
        for r, c in pals:
            copy_g(c, r, mine).start()

    def spread_taps():
        loads[4].wait()
        for p in range(tiles):
            for n, piece in enumerate(turn_rows(fv[:, p * LANES : (p + 1) * LANES].astype(BF16), masks_q)):
                sendf[4 * p + n] = piece
        rxf[me] = sendf[mine]
        for o in range(1, nctx):
            copy_f(flip(me, o), me).start()

    def greet():
        for load in loads[5:]:
            load.wait()
        pl.semaphore_wait(known, 1)

        @pl.when(border)
        def _():
            pl.semaphore_signal(known, inc=1, device_id=at(me, other), device_id_type=MESH)

    def transform(z):
        return jnp.dot(ahead_v[...], jnp.concatenate([z, z], axis=0), preferred_element_type=F32)

    def analyse(whole, rx, sig, rig):
        whole().wait_recv()
        for p in range(0, tiles, 2):
            z = [jnp.concatenate(turn(*[rx[4 * q + n] for n in range(4)], masks_q), axis=0) for q in (p, p + 1)]
            spec = transform(jnp.concatenate(z, axis=1))
            for k in range(2):
                half = spec[:, k * LANES : (k + 1) * LANES]
                sig[p + k] = half
                rig[p + k] = pltpu.roll(half, LANES // 2, 1)

    low, _ = groups(8, F32)
    parity = lax.rem(lax.broadcasted_iota(jnp.int32, (8, LANES), 0), 2)
    alt = jnp.where(parity == 0, 1.0, -1.0).astype(F32)
    zero = jnp.zeros((8, LANES), F32)

    def windows(re, im):
        x_re = [zero] + [sigx[p, re, :] for p in range(tiles)]
        x_im = [zero] + [sigx[p, im, :] for p in range(tiles)]
        r_re = [zero] + [rigx[p, re, :] for p in range(tiles)]
        r_im = [zero] + [rigx[p, im, :] for p in range(tiles)]
        z_re, z_im = [[], []], [[], []]
        for p in range(tiles):
            before_re, before_im = jnp.where(low, r_re[p], r_re[p + 1]), jnp.where(low, r_im[p], r_im[p + 1])
            z_re[0].append(x_re[p + 1] - alt * before_im)
            z_im[0].append(x_im[p + 1] + alt * before_re)
            z_re[1].append(before_re - alt * x_im[p] if p else before_re)
            z_im[1].append(before_im + alt * x_re[p] if p else before_im)
        return z_re, z_im

    def rows_at(i, start):
        return pl.ds(pl.multiple_of(start + i * 8, 8), 8)

    def correlate():
        @pl.loop(0, length // 8, unroll=2)
        def _(i):
            re, im = rows_at(i, 0), rows_at(i, length)
            z_re, z_im = windows(re, im)
            g_re = [sigg[p, re, :] for p in range(tiles)]
            g_im = [sigg[p, im, :] for p in range(tiles)]
            for j in range(nctx):
                b_re, b_im = z_re[j % 2], z_im[j % 2]
                ms = [(m, m - j // 2) for m in range(j // 2, tiles)]
                acc[j, re, :] = total(g_re[m] * b_re[k] + g_im[m] * b_im[k] for m, k in ms)
                acc[j, im, :] = total(g_im[m] * b_re[k] - g_re[m] * b_im[k] for m, k in ms)

        low_f, even_f = groups(64, F32)

        def swing(here, there):
            return pltpu.roll(jnp.where(low_f, here, there), LANES // 2, 1)

        for m in range(0, 2 * length, 64):
            rows = slice(m, m + 64)
            for n in range(nctx // 4):
                a, b, c, d = [acc[4 * n + k, rows, :] for k in range(4)]
                a = jnp.where(low_f, a, c) + swing(c, a)
                b = jnp.where(low_f, b, d) + swing(d, b)
                a = a + pltpu.roll(a, LANES - LANES // 4, 1)
                b = b + pltpu.roll(b, LANES // 4, 1)
                gfs[rows, n * LANES : (n + 1) * LANES] = jnp.where(even_f, a, b).astype(BF16)

    def inverse(high):
        return jnp.dot(back_v[...], jnp.concatenate([high, high], axis=0), preferred_element_type=F32).astype(BF16)

    def send_taps(rows):
        taps = inverse(gfs[...])
        for n in range(nctx // 4):
            for m, piece in enumerate(turn_rows(taps[:, n * LANES : (n + 1) * LANES], masks_q)):
                g2_send[4 * n + m] = piece
        g2_rx[slot] = g2_send[me]
        for r in rows_away:
            copy_g2(me, r, slot).start()
        for r in rows:
            for c in others:
                copy_g2(c, r, slot).start()

    def weigh():
        all_f().wait_recv()
        low_q, even_q = masks_q
        for p in range(tiles):
            z = []
            for k in range(2):
                fa = rxf[2 * p + k]
                turned = pltpu.roll(fa, LANES // 2, 1)
                pieces = []
                for half in (jnp.where(low_q, fa, turned), jnp.where(low_q, turned, fa)):
                    pieces.append(jnp.where(even_q, half, pltpu.roll(half, LANES // 4, 1)))
                    pieces.append(jnp.where(even_q, pltpu.roll(half, LANES - LANES // 4, 1), half))
                z.append(jnp.concatenate(pieces, axis=0))
            wei[p] = transform(jnp.concatenate(z, axis=1))

    def weights(re, im):
        return [[wei[j // 2, rows, pl.ds((j % 2) * LANES, LANES)] for j in range(nctx)] for rows in (re, im)]

    def over_rows(oth, halves):
        @pl.loop(0, length // 16)
        def _(i):
            outs = [halves(rows_at(2 * i + k, 0), rows_at(2 * i + k, length)) for k in range(2)]
            for p in range(tiles):
                for n, start in enumerate((0, length)):
                    rows = pl.ds(pl.multiple_of(start + i * 16, 16), 16)
                    oth[p, rows, :] = jnp.concatenate([outs[0][n][p], outs[1][n][p]], axis=0).astype(BF16)

    def mix_x(re, im):
        w_re, w_im = weights(re, im)
        z_re, z_im = windows(re, im)
        o_re, o_im = [], []
        for p in range(tiles):
            js = [(j, j % 2, p - j // 2) for j in range(2 * p + 2)]
            o_re.append(total(w_re[j] * z_re[h][k] - w_im[j] * z_im[h][k] for j, h, k in js))
            o_im.append(total(w_re[j] * z_im[h][k] + w_im[j] * z_re[h][k] for j, h, k in js))
        return o_re, o_im

    def mix_g(re, im):
        w_re, w_im = weights(re, im)
        g_re = [sigg[p, re, :] for p in range(tiles)]
        g_im = [sigg[p, im, :] for p in range(tiles)]
        r_re = [rigg[p, re, :] for p in range(tiles)] + [zero]
        r_im = [rigg[p, im, :] for p in range(tiles)] + [zero]
        z_re, z_im = [[], []], [[], []]
        for p in range(tiles):
            after_re, after_im = jnp.where(low, r_re[p], r_re[p + 1]), jnp.where(low, r_im[p], r_im[p + 1])
            z_re[0].append(g_re[p] + alt * after_im)
            z_im[0].append(g_im[p] - alt * after_re)
            z_re[1].append(after_re + alt * g_im[p + 1] if p + 1 < tiles else after_re)
            z_im[1].append(after_im - alt * g_re[p + 1] if p + 1 < tiles else after_im)
        o_re, o_im = [], []
        for p in range(tiles):
            js = [(j, j % 2, p + j // 2) for j in range(2 * (tiles - p))]
            o_re.append(total(w_re[j] * z_re[h][k] + w_im[j] * z_im[h][k] for j, h, k in js))
            o_im.append(total(w_re[j] * z_im[h][k] - w_im[j] * z_re[h][k] for j, h, k in js))
        return o_re, o_im

    def give_back(oth, send, rx, copy):
        for p in range(0, tiles, 2):
            both = inverse(jnp.concatenate([oth[p], oth[p + 1]], axis=1))
            for k in range(2):
                for n, piece in enumerate(turn_rows(both[:, k * LANES : (k + 1) * LANES], masks_q)):
                    send[4 * (p + k) + n] = piece
        rx[mine] = send[mine]
        for c in others:
            copy(c, row, mine).start()
            copy(c, other, mine).start()
        copy(me, other, mine).start()

    early = row < ndp // 2

    @pl.when(early)
    def _():
        spread_taps()
        spread_grads()
        greet()
        analyse(all_x, rxx, sigx, rigx)
        weigh()
        over_rows(othx, mix_x)
        give_back(othx, mx_send, mx_rx, copy_mx)
        analyse(all_g, rxg, sigg, rigg)
        over_rows(othg, mix_g)
        give_back(othg, mg_send, mg_rx, copy_mg)
        correlate()
        send_taps(list(range(ndp // 2, ndp)) + list(range(ndp // 2)))

    @pl.when(jnp.logical_not(early))
    def _():
        spread_grads()
        spread_taps()
        greet()
        analyse(all_x, rxx, sigx, rigx)
        analyse(all_g, rxg, sigg, rigg)
        correlate()
        send_taps(range(ndp))
        weigh()
        over_rows(othx, mix_x)
        give_back(othx, mx_send, mx_rx, copy_mx)
        over_rows(othg, mix_g)
        give_back(othg, mg_send, mg_rx, copy_mg)

    for whole in (all_mx, all_mg, all_g2):
        whole().wait_recv()
    for whole in (all_x, all_g, all_f, all_mx, all_mg, all_g2):
        whole().wait_send()


def finish(mx, mg, g2, q, k, v, g, out_hbm, gq_hbm, gk_hbm, gv_hbm, gf_hbm, out_v, gq_v, gk_v, gv_v, gf_v, sems):
    length = q.shape[1]
    ql = length // 4
    tiles = mg.shape[0] // 4
    masks_q, masks_f = groups(ql, BF16), groups(ql, F32)

    pairs = ((out_v, out_hbm), (gq_v, gq_hbm), (gk_v, gk_hbm), (gv_v, gv_hbm), (gf_v, gf_hbm))
    for p in range(tiles):
        cols = slice(p * LANES, (p + 1) * LANES)
        mixed, back = [
            jnp.concatenate(turn(*[m[4 * p + n] for n in range(4)], masks_q), axis=0).astype(F32) for m in (mx, mg)
        ]
        out_v[0, :, cols] = (q[0, :, cols].astype(F32) * mixed).astype(BF16)
        gq_v[0, :, cols] = (g[0, :, cols].astype(F32) * mixed).astype(BF16)
        gk_v[0, :, cols] = (v[0, :, cols].astype(F32) * back).astype(BF16)
        gv_v[0, :, cols] = (k[0, :, cols].astype(F32) * back).astype(BF16)
        quads = [g2[4 * p + n].astype(F32) + g2[4 * (tiles + p) + n].astype(F32) for n in range(4)]
        for n, piece in enumerate(turn(*quads, masks_f)):
            gf_v[n * ql : (n + 1) * ql, cols] = piece
        for n, (src, dst) in enumerate(pairs):
            part = (slice(None),) * (len(src.shape) - 1) + (cols,)
            pltpu.make_async_copy(src.at[part], dst.at[part], sems.at[n]).start()
    for n, (src, dst) in enumerate(pairs):
        pltpu.make_async_copy(src, dst, sems.at[n]).wait()


def fused(nctx, ndp, query, key_input, value_input, filter_taps, grad_output):
    length, channels = query.shape[1], query.shape[2]
    ahead, back = block_tables(length)
    vm = pl.BlockSpec(memory_space=pltpu.VMEM)
    hbm = pl.BlockSpec(memory_space=pltpu.HBM)
    ql, tiles = length // 4, nctx // 2
    dma = pltpu.SemaphoreType.DMA
    kept = 2 * (4 * query.size + (4 * nctx + ndp * nctx) * ql * LANES) + 16384
    pieces = pltpu.VMEM((2 * nctx, ql, LANES), BF16)
    spectrum = pltpu.VMEM((tiles, 2 * length, LANES), F32)
    arrived = pl.pallas_call(
        functools.partial(kernel, nctx, ndp),
        out_shape=(
            pieces,
            pieces,
            pltpu.VMEM((ndp * nctx, ql, LANES), BF16),
            pltpu.VMEM(query.shape, BF16),
            pltpu.VMEM(query.shape, BF16),
            pltpu.VMEM(query.shape, BF16),
            pltpu.VMEM(query.shape, BF16),
        ),
        in_specs=[hbm] * 7,
        out_specs=(vm,) * 7,
        scratch_shapes=[
            pltpu.VMEM((length, channels), F32),
            pltpu.VMEM(ahead.shape, BF16),
            pltpu.VMEM(back.shape, BF16),
            pieces,
            pieces,
            pieces,
            pieces,
            pieces,
            pltpu.VMEM((nctx, ql, LANES), BF16),
            spectrum,
            spectrum,
            spectrum,
            spectrum,
            pltpu.VMEM((tiles, 2 * length, 2 * LANES), F32),
            pltpu.VMEM((tiles, 2 * length, LANES), BF16),
            pltpu.VMEM((tiles, 2 * length, LANES), BF16),
            pltpu.VMEM((nctx, 2 * length, LANES), F32),
            pltpu.VMEM((2 * length, nctx // 4 * LANES), BF16),
            pltpu.VMEM((nctx, ql, LANES), BF16),
            pieces,
            pieces,
            pltpu.SemaphoreType.REGULAR,
            dma((7,)),
        ]
        + [dma] * 12,
        compiler_params=pltpu.CompilerParams(
            collective_id=0, has_side_effects=True, vmem_limit_bytes=VMEM_BYTES - kept
        ),
    )(query, key_input, value_input, filter_taps, grad_output, jnp.asarray(ahead), jnp.asarray(back))
    wide = jax.ShapeDtypeStruct(query.shape, BF16)
    return pl.pallas_call(
        finish,
        out_shape=(wide, wide, wide, wide, jax.ShapeDtypeStruct((length, channels), F32)),
        in_specs=[vm] * 7,
        out_specs=(hbm,) * 5,
        scratch_shapes=[pltpu.VMEM(query.shape, BF16)] * 4 + [pltpu.VMEM((length, channels), F32), dma((5,))],
        compiler_params=pltpu.CompilerParams(vmem_limit_bytes=16 * 1024 * 1024),
    )(*arrived)


def build_tables(length):
    padded = 2 * length
    columns = 1
    while columns * columns < padded and length % (2 * columns) == 0:
        columns = columns * 2
    row_count = padded // columns
    col_index = jnp.arange(columns, dtype=jnp.int32)
    row_index = jnp.arange(row_count, dtype=jnp.int32)
    col_angle = (col_index[:, None] * col_index[None, :] % columns).astype(jnp.float32) * (
        2.0 * math.pi / columns
    )
    row_angle = (row_index[:, None] * row_index[None, :] % row_count).astype(jnp.float32) * (
        2.0 * math.pi / row_count
    )
    twist_angle = (row_index[:, None] * col_index[None, :] % padded).astype(jnp.float32) * (
        2.0 * math.pi / padded
    )
    return (
        jnp.cos(col_angle),
        -jnp.sin(col_angle),
        jnp.cos(row_angle),
        -jnp.sin(row_angle),
        jnp.cos(twist_angle),
        -jnp.sin(twist_angle),
        row_count,
        columns,
        padded,
    )


def forward(signal, tables):
    col_real, col_imag, row_real, row_imag, twist_real, twist_imag, row_count, columns, padded = (
        tables
    )
    half_rows = row_count // 2
    blocks = signal.reshape(signal.shape[0], half_rows, columns, signal.shape[2])
    section_real = jnp.einsum("kn,snac->scka", row_real[:, :half_rows], blocks, precision=HIGH)
    section_imag = jnp.einsum("kn,snac->scka", row_imag[:, :half_rows], blocks, precision=HIGH)
    turned_real = section_real * twist_real - section_imag * twist_imag
    turned_imag = section_real * twist_imag + section_imag * twist_real
    spec_real = jnp.einsum("scka,aj->sckj", turned_real, col_real, precision=HIGH) - jnp.einsum(
        "scka,aj->sckj", turned_imag, col_imag, precision=HIGH
    )
    spec_imag = jnp.einsum("scka,aj->sckj", turned_real, col_imag, precision=HIGH) + jnp.einsum(
        "scka,aj->sckj", turned_imag, col_real, precision=HIGH
    )
    return (spec_real, spec_imag)


def inverse(spec, tables):
    col_real, col_imag, row_real, row_imag, twist_real, twist_imag, row_count, columns, padded = (
        tables
    )
    spec_real, spec_imag = spec
    half_rows = row_count // 2
    section_real = jnp.einsum("scka,aj->sckj", spec_real, col_real, precision=HIGH) + jnp.einsum(
        "scka,aj->sckj", spec_imag, col_imag, precision=HIGH
    )
    section_imag = jnp.einsum("scka,aj->sckj", spec_imag, col_real, precision=HIGH) - jnp.einsum(
        "scka,aj->sckj", spec_real, col_imag, precision=HIGH
    )
    turned_real = section_real * twist_real + section_imag * twist_imag
    turned_imag = section_imag * twist_real - section_real * twist_imag
    signal = jnp.einsum(
        "nk,scka->snac", row_real[:half_rows], turned_real, precision=HIGH
    ) + jnp.einsum("nk,scka->snac", row_imag[:half_rows], turned_imag, precision=HIGH)
    return signal.reshape(signal.shape[0], half_rows * columns, signal.shape[3]) * (1.0 / padded)


def times_spec(first, second):
    return (
        first[0] * second[0] - first[1] * second[1],
        first[0] * second[1] + first[1] * second[0],
    )


def times_conj(first, second):
    return (
        first[0] * second[0] + first[1] * second[1],
        first[1] * second[0] - first[0] * second[1],
    )


def local(query, key_input, value_input, filter_taps, grad_output):
    product = (key_input.astype(jnp.float32) * value_input.astype(jnp.float32)).astype(jnp.bfloat16)
    grad_mix = (grad_output.astype(jnp.float32) * query.astype(jnp.float32)).astype(jnp.bfloat16)
    owned_filter = lax.all_to_all(filter_taps, "ctx", split_axis=1, concat_axis=0, tiled=True)
    tables = build_tables(owned_filter.shape[0])
    filter_spec = forward(owned_filter[None], tables)
    local_product = lax.all_to_all(product, "ctx", split_axis=2, concat_axis=1, tiled=True)
    prod_spec = forward(local_product.astype(jnp.float32), tables)
    owned_mixed = inverse(times_spec(filter_spec, prod_spec), tables).astype(jnp.bfloat16)
    owned_mixed, prod_spec = (owned_mixed, prod_spec)
    mixed = lax.all_to_all(owned_mixed, "ctx", split_axis=1, concat_axis=2, tiled=True)
    owned_grad = lax.all_to_all(grad_mix, "ctx", split_axis=2, concat_axis=1, tiled=True)
    grad_spec = forward(owned_grad.astype(jnp.float32), tables)
    owned_back = inverse(times_conj(grad_spec, filter_spec), tables).astype(jnp.bfloat16)
    taps_spec = times_conj(grad_spec, prod_spec)
    owned_back, taps_spec = (
        owned_back,
        (jnp.sum(taps_spec[0], axis=0), jnp.sum(taps_spec[1], axis=0)),
    )
    grad_product = lax.all_to_all(owned_back, "ctx", split_axis=1, concat_axis=2, tiled=True)
    mixed_wide = mixed.astype(jnp.float32)
    back_wide = grad_product.astype(jnp.float32)
    output = (query.astype(jnp.float32) * mixed_wide).astype(jnp.bfloat16)
    grad_query = (grad_output.astype(jnp.float32) * mixed_wide).astype(jnp.bfloat16)
    grad_key = (back_wide * value_input.astype(jnp.float32)).astype(jnp.bfloat16)
    grad_value = (back_wide * key_input.astype(jnp.float32)).astype(jnp.bfloat16)
    local_taps = inverse((taps_spec[0][None], taps_spec[1][None]), tables)[0]
    owned_taps = lax.psum(local_taps, "dp")
    grad_filter = lax.all_to_all(owned_taps, "ctx", split_axis=0, concat_axis=1, tiled=True)
    return (output, grad_query, grad_key, grad_value, grad_filter)


def plan(mesh, query, key_input, value_input, filter_taps, grad_output):
    nctx, ndp = mesh.shape["ctx"], mesh.shape["dp"]
    sequences, length, channels = query.shape
    paired = nctx == 2 * ndp and ndp // 2 == 2
    fits = paired and 2 * channels == nctx * LANES and sequences == 1 and length % 64 == 0 and length <= LANES
    run = functools.partial(fused, nctx, ndp) if fits else local
    return run(query, key_input, value_input, filter_taps, grad_output)


def solution(mesh):
    wide, taps = P("dp", "ctx", None), P("ctx", None)
    return jax.shard_map(
        functools.partial(plan, mesh),
        mesh=mesh,
        in_specs=(wide, wide, wide, taps, wide),
        out_specs=(wide, wide, wide, wide, taps),
        check_vma=False,
    )
```

time: 24.1 us -> 23 us (0.954)
  Pallas kernels: 23.3 us -> 22.2 us
    pallas_call x1, Pallas kernels: 22.2 us -> 20.9 us  [fused(): pl.pallas_call(functools.partial(kernel, nctx, ndp), out_shape=(pieces, p...]
where the time goes in v1:
time: 23 us; the launch traced here: 22.9 us
  Pallas kernels  22.2 us (97%)
  between operations  0.64 us (3%)
    pallas_call x1, Pallas kernels, fused(): pl.pallas_call(functools.partial(kernel, nctx, ndp), out_shape=(pieces, p...  20.9 us
    pallas_call x1, Pallas kernels, fused(): pl.pallas_call(finish, out_shape=(wide, wide, wide, wide, jax.ShapeDtypeS...  1.32 us

profile of v1, /device:TPU:0, one launch (start us, length us, event | category | flops | bytes accessed | tf_op | source)
XLA Modules:
  0.0 22.9 jit_solution(13190193845254487598)
XLA Ops:
  0.6 20.9 %shard_map.110 = (bf16[16,32,128]{2,1,0:T(8,128)(2,1)S(1)}, bf16[16,32,128]{2,1,0:T(8,128)(2,1)S(1)}, bf16[32,32,128]{2,1,0:T(8,128)(2,1)S(1)}, bf16[1,128,512]{...) custom-call(bf16[1,128,512]{2,1,0:T(8,128)(2,1)} %q_hbm.1, ...), custom_call_target="tpu_custom_call" | custom-call | tf_op jit(solution)/shard_map/pallas_call | solution.py:478
  21.6 1.3 %shard_map.111 = (bf16[1,128,512]{2,1,0:T(8,128)(2,1)}, bf16[1,128,512]{2,1,0:T(8,128)(2,1)}, bf16[1,128,512]{2,1,0:T(8,128)(2,1)}, bf16[1,128,512]{2,1,0:T(8,128)(2,1)}, f32[128,512]{1,0:T(8,128)}) custom-call(bf16[16,32,128]{2,1,0:T(8,128)(2,1)S(1)} %get-tuple-element.12.mx, bf16[16,32,128]{2,1,0:T(8,128)(2,1)S(1)} %get-tuple-element.13.mg, ...), custom_call_target="tpu_custom_call" | custom-call | tf_op jit(solution)/shard_map/pallas_call | solution.py:522

commit v2 on v1

--- a/solution.py
+++ b/solution.py
@@ -93,9 +93,13 @@
     g_hbm,
     ahead_hbm,
     back_hbm,
+    g2_rx,
+    out_v,
+    gq_v,
+    gk_v,
+    gv_v,
     mx_rx,
     mg_rx,
-    g2_rx,
     qv,
     kv,
     vv,
@@ -131,6 +135,9 @@
     f_rsem,
     g2_ssem,
     g2_rsem,
+    own_rsem,
+    fwd_ssem,
+    fwd_rsem,
     mx_ssem,
     mx_rsem,
     mg_ssem,
@@ -145,13 +152,11 @@
     base = row - part
     other = base + 1 - part
     mine = 2 * me + part
-    slot = (row // 2) * 2 * nctx + mine
+    slot = row * nctx + me
+    early = row < ndp // 2
 
     pairs = ((k_hbm, kv), (v_hbm, vv), (g_hbm, gv), (q_hbm, qv), (f_hbm, fv), (ahead_hbm, ahead_v), (back_hbm, back_v))
     loads = [pltpu.make_async_copy(src, dst, load_sem.at[n]) for n, (src, dst) in enumerate(pairs)]
-    for load in loads:
-        load.start()
-
     def at(ctx, dp):
         return {"ctx": ctx, "dp": dp}
 
@@ -161,13 +166,19 @@
     border = jnp.logical_or(inner, outer)
     barrier = pltpu.get_barrier_semaphore()
     pals = [(other, me)] + [(r, flip(me, o)) for o in range(1, nctx) for r in (row, other)]
-    for r, c in pals:
+    for r, c in reversed(pals):
         pl.semaphore_signal(barrier, inc=1, device_id=at(c, r), device_id_type=MESH)
 
     @pl.when(border)
     def _():
         pl.semaphore_signal(barrier, inc=1, device_id=at(me, across), device_id_type=MESH)
 
+    for p in range(tiles):
+        cols = slice(p * LANES, (p + 1) * LANES)
+        for n, (src, dst) in enumerate(pairs[:2]):
+            pltpu.make_async_copy(src.at[:, :, cols], dst.at[:, :, cols], load_sem.at[n]).start()
+    for load in loads[2:]:
+        load.start()
     masks_q = groups(ql, BF16)
 
     def prepare(a_ref, b_ref, into):
@@ -207,17 +218,21 @@
     def copy_f(ctx, into):
         return remote(sendf.at[2 * ctx + part], rxf.at[into], f_ssem, f_rsem, ctx, row)
 
-    def copy_g2(ctx, dp, into):
-        return remote(g2_send.at[ctx], g2_rx.at[into], g2_ssem, g2_rsem, ctx, dp)
+    def copy_g2(ctx, dp, rsem):
+        return remote(g2_send.at[ctx], g2_rx.at[slot], g2_ssem, rsem, ctx, dp)
+
+    def wait_g2(rsem, count):
+        every = pl.ds(0, count)
+        return remote(g2_rx.at[every], g2_rx.at[every], g2_ssem, rsem, me, other)
+
+    def forward(dp):
+        block = pl.ds(pl.multiple_of(dp * nctx, nctx), nctx)
+        return remote(g2_rx.at[block], g2_rx.at[block], fwd_ssem, fwd_rsem, me, other)
 
     def all_f():
         every = pl.ds(0, nctx - 1)
         return remote(sendf.at[every], rxf.at[every], f_ssem, f_rsem, me, other)
 
-    def all_g2():
-        every = pl.ds(0, nctx * ndp - 1)
-        return remote(g2_rx.at[every], g2_rx.at[every], g2_ssem, g2_rsem, me, other)
-
     for r, c in pals:
         copy_x(c, r, mine).start()
 
@@ -226,7 +241,6 @@
         pl.semaphore_signal(known, inc=1, device_id=at(me, across), device_id_type=MESH)
 
     others = [k + jnp.where(me <= k, 1, 0) for k in range(nctx - 1)]
-    rows_away = [k + jnp.where(row <= k, 1, 0) for k in range(ndp - 1)]
 
     def spread_grads():
         for load in loads[2:4]:
@@ -257,15 +271,20 @@
     def transform(z):
         return jnp.dot(ahead_v[...], jnp.concatenate([z, z], axis=0), preferred_element_type=F32)
 
-    def analyse(whole, rx, sig, rig):
+    def analyse(whole, rx, sig, rig=None):
         whole().wait_recv()
+        z = [jnp.concatenate(turn(*[rx[4 * p + n] for n in range(4)], masks_q), axis=0) for p in range(tiles)]
         for p in range(0, tiles, 2):
-            z = [jnp.concatenate(turn(*[rx[4 * q + n] for n in range(4)], masks_q), axis=0) for q in (p, p + 1)]
-            spec = transform(jnp.concatenate(z, axis=1))
+            spec = transform(jnp.concatenate(z[p : p + 2], axis=1))
             for k in range(2):
                 half = spec[:, k * LANES : (k + 1) * LANES]
                 sig[p + k] = half
-                rig[p + k] = pltpu.roll(half, LANES // 2, 1)
+                if rig is not None:
+                    rig[p + k] = pltpu.roll(half, LANES // 2, 1)
+
+    def swap_grads():
+        for p in range(tiles):
+            rigg[p] = pltpu.roll(sigg[p], LANES // 2, 1)
 
     low, _ = groups(8, F32)
     parity = lax.rem(lax.broadcasted_iota(jnp.int32, (8, LANES), 0), 2)
@@ -307,45 +326,55 @@
         def swing(here, there):
             return pltpu.roll(jnp.where(low_f, here, there), LANES // 2, 1)
 
-        for m in range(0, 2 * length, 64):
-            rows = slice(m, m + 64)
-            for n in range(nctx // 4):
-                a, b, c, d = [acc[4 * n + k, rows, :] for k in range(4)]
-                a = jnp.where(low_f, a, c) + swing(c, a)
-                b = jnp.where(low_f, b, d) + swing(d, b)
-                a = a + pltpu.roll(a, LANES - LANES // 4, 1)
-                b = b + pltpu.roll(b, LANES // 4, 1)
-                gfs[rows, n * LANES : (n + 1) * LANES] = jnp.where(even_f, a, b).astype(BF16)
+        chunks = [(n, slice(m, m + 64)) for m in range(0, 2 * length, 64) for n in range(nctx // 4)]
+        for n, rows in chunks:
+            for k in (0, 2):
+                a, b = acc[4 * n + k, rows, :], acc[4 * n + k + 1, rows, :]
+                moved = pltpu.roll(jnp.where(even_f, b, a), LANES // 4, 1)
+                acc[4 * n + k, rows, :] = jnp.where(even_f, a, b) + moved
+        for n, rows in chunks:
+            a, b = acc[4 * n, rows, :], acc[4 * n + 2, rows, :]
+            gfs[rows, n * LANES : (n + 1) * LANES] = (jnp.where(low_f, a, b) + swing(b, a)).astype(BF16)
 
     def inverse(high):
         return jnp.dot(back_v[...], jnp.concatenate([high, high], axis=0), preferred_element_type=F32).astype(BF16)
 
-    def send_taps(rows):
+    def send_taps(dp, rsem, here=False):
+        for c in others:
+            copy_g2(c, dp, rsem).start()
+        if not here:
+            copy_g2(me, dp, rsem).start()
+
+    def send_pair(index):
+        @pl.when(part == index)
+        def _():
+            send_taps(row, g2_rsem, True)
+
+        @pl.when(part != index)
+        def _():
+            send_taps(other, g2_rsem)
+
+    def finish_taps():
         taps = inverse(gfs[...])
         for n in range(nctx // 4):
             for m, piece in enumerate(turn_rows(taps[:, n * LANES : (n + 1) * LANES], masks_q)):
                 g2_send[4 * n + m] = piece
         g2_rx[slot] = g2_send[me]
-        for r in rows_away:
-            copy_g2(me, r, slot).start()
-        for r in rows:
-            for c in others:
-                copy_g2(c, r, slot).start()
 
     def weigh():
         all_f().wait_recv()
         low_q, even_q = masks_q
-        for p in range(tiles):
-            z = []
-            for k in range(2):
-                fa = rxf[2 * p + k]
-                turned = pltpu.roll(fa, LANES // 2, 1)
-                pieces = []
-                for half in (jnp.where(low_q, fa, turned), jnp.where(low_q, turned, fa)):
-                    pieces.append(jnp.where(even_q, half, pltpu.roll(half, LANES // 4, 1)))
-                    pieces.append(jnp.where(even_q, pltpu.roll(half, LANES - LANES // 4, 1), half))
-                z.append(jnp.concatenate(pieces, axis=0))
-            wei[p] = transform(jnp.concatenate(z, axis=1))
+        z = []
+        for c in range(nctx):
+            fa = rxf[c]
+            turned = pltpu.roll(fa, LANES // 2, 1)
+            pieces = []
+            for half in (jnp.where(low_q, fa, turned), jnp.where(low_q, turned, fa)):
+                pieces.append(jnp.where(even_q, half, pltpu.roll(half, LANES // 4, 1)))
+                pieces.append(jnp.where(even_q, pltpu.roll(half, LANES - LANES // 4, 1), half))
+            z.append(jnp.concatenate(pieces, axis=0))
+        for p in range(tiles):
+            wei[p] = transform(jnp.concatenate(z[2 * p : 2 * p + 2], axis=1))
 
     def weights(re, im):
         return [[wei[j // 2, rows, pl.ds((j % 2) * LANES, LANES)] for j in range(nctx)] for rows in (re, im)]
@@ -390,18 +419,15 @@
         return o_re, o_im
 
     def give_back(oth, send, rx, copy):
-        for p in range(0, tiles, 2):
-            both = inverse(jnp.concatenate([oth[p], oth[p + 1]], axis=1))
-            for k in range(2):
-                for n, piece in enumerate(turn_rows(both[:, k * LANES : (k + 1) * LANES], masks_q)):
-                    send[4 * (p + k) + n] = piece
+        wide = [inverse(jnp.concatenate([oth[p], oth[p + 1]], axis=1)) for p in range(0, tiles, 2)]
+        for p in range(tiles):
+            for n, piece in enumerate(turn_rows(wide[p // 2][:, p % 2 * LANES : (p % 2 + 1) * LANES], masks_q)):
+                send[4 * p + n] = piece
         rx[mine] = send[mine]
         for c in others:
             copy(c, row, mine).start()
             copy(c, other, mine).start()
         copy(me, other, mine).start()
-
-    early = row < ndp // 2
 
     @pl.when(early)
     def _():
@@ -416,7 +442,11 @@
         over_rows(othg, mix_g)
         give_back(othg, mg_send, mg_rx, copy_mg)
         correlate()
-        send_taps(list(range(ndp // 2, ndp)) + list(range(ndp // 2)))
+        finish_taps()
+        send_pair(0)
+        for dp in range(ndp // 2, ndp):
+            send_taps(dp, g2_rsem)
+        send_pair(1)
 
     @pl.when(jnp.logical_not(early))
     def _():
@@ -424,45 +454,69 @@
         spread_taps()
         greet()
         analyse(all_x, rxx, sigx, rigx)
-        analyse(all_g, rxg, sigg, rigg)
+        analyse(all_g, rxg, sigg)
         correlate()
-        send_taps(range(ndp))
+        finish_taps()
+        for dp in range(ndp // 2):
+            send_taps(dp, g2_rsem)
+        send_taps(row, own_rsem, True)
         weigh()
+        swap_grads()
         over_rows(othx, mix_x)
         give_back(othx, mx_send, mx_rx, copy_mx)
         over_rows(othg, mix_g)
         give_back(othg, mg_send, mg_rx, copy_mg)
-
-    for whole in (all_mx, all_mg, all_g2):
-        whole().wait_recv()
-    for whole in (all_x, all_g, all_f, all_mx, all_mg, all_g2):
+        wait_g2(own_rsem, nctx - 1).wait_recv()
+        forward(row).start()
+
+    def gate(rx, first, first_out, second, second_out):
+        for p in range(tiles):
+            cols = slice(p * LANES, (p + 1) * LANES)
+            value = jnp.concatenate(turn(*[rx[4 * p + n] for n in range(4)], masks_q), axis=0).astype(F32)
+            first_out[0, :, cols] = (first[0, :, cols].astype(F32) * value).astype(BF16)
+            second_out[0, :, cols] = (second[0, :, cols].astype(F32) * value).astype(BF16)
+
+    all_mx().wait_recv()
+    gate(mx_rx, qv, out_v, gv, gq_v)
+    all_mg().wait_recv()
+    gate(mg_rx, vv, gk_v, kv, gv_v)
+
+    @pl.when(early)
+    def _():
+        wait_g2(g2_rsem, ndp * nctx - 1).wait_recv()
+        wait_g2(g2_rsem, ndp * nctx - 1).wait_send()
+
+    @pl.when(jnp.logical_not(early))
+    def _():
+        wait_g2(g2_rsem, ndp // 2 * nctx).wait_recv()
+        wait_g2(fwd_rsem, nctx).wait_recv()
+        forward(row).wait_send()
+        wait_g2(g2_rsem, (ndp // 2 + 1) * nctx - 1).wait_send()
+
+    for whole in (all_x, all_g, all_f, all_mx, all_mg):
         whole().wait_send()
 
 
-def finish(mx, mg, g2, q, k, v, g, out_hbm, gq_hbm, gk_hbm, gv_hbm, gf_hbm, out_v, gq_v, gk_v, gv_v, gf_v, sems):
-    length = q.shape[1]
-    ql = length // 4
-    tiles = mg.shape[0] // 4
-    masks_q, masks_f = groups(ql, BF16), groups(ql, F32)
-
-    pairs = ((out_v, out_hbm), (gq_v, gq_hbm), (gk_v, gk_hbm), (gv_v, gv_hbm), (gf_v, gf_hbm))
+def finish(g2, out, gq, gk, gv, out_hbm, gq_hbm, gk_hbm, gv_hbm, gf_hbm, gf_v, sems):
+    length, channels = gf_v.shape
+    ql, tiles = length // 4, channels // LANES
+    copies = []
+    for n, (src, dst) in enumerate(((out, out_hbm), (gq, gq_hbm), (gk, gk_hbm), (gv, gv_hbm), (gf_v, gf_hbm))):
+        copies.append(pltpu.make_async_copy(src, dst, sems.at[n]))
+    for copy in copies[:4]:
+        copy.start()
+    masks_f = groups(ql, F32)
     for p in range(tiles):
         cols = slice(p * LANES, (p + 1) * LANES)
-        mixed, back = [
-            jnp.concatenate(turn(*[m[4 * p + n] for n in range(4)], masks_q), axis=0).astype(F32) for m in (mx, mg)
+        quads = [
+            total(g2[2 * tiles * (2 * q + n % 2) + 2 * p + n // 2].astype(F32) for q in range(g2.shape[0] // (4 * tiles)))
+            for n in range(4)
         ]
-        out_v[0, :, cols] = (q[0, :, cols].astype(F32) * mixed).astype(BF16)
-        gq_v[0, :, cols] = (g[0, :, cols].astype(F32) * mixed).astype(BF16)
-        gk_v[0, :, cols] = (v[0, :, cols].astype(F32) * back).astype(BF16)
-        gv_v[0, :, cols] = (k[0, :, cols].astype(F32) * back).astype(BF16)
-        quads = [g2[4 * p + n].astype(F32) + g2[4 * (tiles + p) + n].astype(F32) for n in range(4)]
         for n, piece in enumerate(turn(*quads, masks_f)):
             gf_v[n * ql : (n + 1) * ql, cols] = piece
-        for n, (src, dst) in enumerate(pairs):
-            part = (slice(None),) * (len(src.shape) - 1) + (cols,)
-            pltpu.make_async_copy(src.at[part], dst.at[part], sems.at[n]).start()
-    for n, (src, dst) in enumerate(pairs):
-        pltpu.make_async_copy(src, dst, sems.at[n]).wait()
+        pltpu.make_async_copy(gf_v.at[:, cols], gf_hbm.at[:, cols], sems.at[4]).start()
+    for copy in copies:
+        copy.wait()
 
 
 def fused(nctx, ndp, query, key_input, value_input, filter_taps, grad_output):
@@ -472,23 +526,21 @@
     hbm = pl.BlockSpec(memory_space=pltpu.HBM)
     ql, tiles = length // 4, nctx // 2
     dma = pltpu.SemaphoreType.DMA
-    kept = 2 * (4 * query.size + (4 * nctx + ndp * nctx) * ql * LANES) + 16384
+    kept = 2 * (4 * query.size + ndp * nctx * ql * LANES) + 16384
     pieces = pltpu.VMEM((2 * nctx, ql, LANES), BF16)
     spectrum = pltpu.VMEM((tiles, 2 * length, LANES), F32)
     arrived = pl.pallas_call(
         functools.partial(kernel, nctx, ndp),
-        out_shape=(
-            pieces,
-            pieces,
-            pltpu.VMEM((ndp * nctx, ql, LANES), BF16),
+        out_shape=(pltpu.VMEM((ndp * nctx, ql, LANES), BF16),) + (pltpu.VMEM(query.shape, BF16),) * 4,
+        in_specs=[hbm] * 7,
+        out_specs=(vm,) * 5,
+        scratch_shapes=[
+            pieces,
+            pieces,
             pltpu.VMEM(query.shape, BF16),
             pltpu.VMEM(query.shape, BF16),
             pltpu.VMEM(query.shape, BF16),
             pltpu.VMEM(query.shape, BF16),
-        ),
-        in_specs=[hbm] * 7,
-        out_specs=(vm,) * 7,
-        scratch_shapes=[
             pltpu.VMEM((length, channels), F32),
             pltpu.VMEM(ahead.shape, BF16),
             pltpu.VMEM(back.shape, BF16),
@@ -513,7 +565,7 @@
             pltpu.SemaphoreType.REGULAR,
             dma((7,)),
         ]
-        + [dma] * 12,
+        + [dma] * 15,
         compiler_params=pltpu.CompilerParams(
             collective_id=0, has_side_effects=True, vmem_limit_bytes=VMEM_BYTES - kept
         ),
@@ -522,9 +574,9 @@
     return pl.pallas_call(
         finish,
         out_shape=(wide, wide, wide, wide, jax.ShapeDtypeStruct((length, channels), F32)),
-        in_specs=[vm] * 7,
+        in_specs=[vm] * 5,
         out_specs=(hbm,) * 5,
-        scratch_shapes=[pltpu.VMEM(query.shape, BF16)] * 4 + [pltpu.VMEM((length, channels), F32), dma((5,))],
+        scratch_shapes=[pltpu.VMEM((length, channels), F32), dma((5,))],
         compiler_params=pltpu.CompilerParams(vmem_limit_bytes=16 * 1024 * 1024),
     )(*arrived)
 

time: 23 us -> 22.7 us (0.987)
  Pallas kernels: 22.2 us -> 21.9 us
    pallas_call x1, Pallas kernels: 1.32 us -> 0.91 us  [fused(): pl.pallas_call(finish, out_shape=(wide, wide, wide, wide, jax.ShapeDtypeS...]
where the time goes in v2:
time: 22.7 us; the launch traced here: 22.5 us
  Pallas kernels  21.9 us (96%)
  between operations  0.64 us (3%)
    pallas_call x1, Pallas kernels, fused(): pl.pallas_call(functools.partial(kernel, nctx, ndp), out_shape=(pltpu.VME...  21 us
    pallas_call x1, Pallas kernels, fused(): pl.pallas_call(finish, out_shape=(wide, wide, wide, wide, jax.ShapeDtypeS...  0.91 us

profile of v2, /device:TPU:0, one launch (start us, length us, event | category | flops | bytes accessed | tf_op | source)
XLA Modules:
  0.0 22.5 jit_solution(4146814496027731159)
XLA Ops:
  0.6 21.0 %shard_map.110 = (bf16[32,32,128]{2,1,0:T(8,128)(2,1)S(1)}, bf16[1,128,512]{2,1,0:T(8,128)(2,1)S(1)}, bf16[1,128,512]{2,1,0:T(8,128)(2,1)S(1)}, bf16[1,128,512]{2,1,0:T(8,128)(2,1)S(1)}, bf16[1,128,512]{2,1,0:T(8,128)(2,1)S(1)}) custom-call(bf16[1,128,512]{2,1,0:T(8,128)(2,1)} %q_hbm.1, bf16[1,128,512]{2,1,0:T(8,128)(2,1)} %k_hbm.1, ...), custom_call_target="tpu_custom_call" | custom-call | tf_op jit(solution)/shard_map/pallas_call | solution.py:532
  21.6 0.9 %shard_map.111 = (bf16[1,128,512]{2,1,0:T(8,128)(2,1)}, bf16[1,128,512]{2,1,0:T(8,128)(2,1)}, bf16[1,128,512]{2,1,0:T(8,128)(2,1)}, bf16[1,128,512]{2,1,0:T(8,128)(2,1)}, f32[128,512]{1,0:T(8,128)}) custom-call(bf16[32,32,128]{2,1,0:T(8,128)(2,1)S(1)} %get-tuple-element.10.g2, bf16[1,128,512]{2,1,0:T(8,128)(2,1)S(1)} %get-tuple-element.11.out, ...), custom_call_target="tpu_custom_call" | custom-call | tf_op jit(solution)/shard_map/pallas_call | solution.py:574

commit v3 on v2

--- a/solution.py
+++ b/solution.py
@@ -30,10 +30,10 @@
 
     with jax.ensure_compile_time_eval():
         ahead_high, ahead_low = split(ahead)
-        back_high, back_low = split(back)
+        back_high, _ = split(back)
         return (
             np.asarray(jnp.concatenate([ahead_high, ahead_low], axis=1)),
-            np.asarray(jnp.concatenate([back_high, back_low], axis=1)),
+            np.asarray(back_high),
         )
 
 
@@ -179,7 +179,7 @@
             pltpu.make_async_copy(src.at[:, :, cols], dst.at[:, :, cols], load_sem.at[n]).start()
     for load in loads[2:]:
         load.start()
-    masks_q = groups(ql, BF16)
+    masks_q, masks_w = groups(ql, BF16), groups(length, BF16)
 
     def prepare(a_ref, b_ref, into):
         for p in range(tiles):
@@ -271,34 +271,40 @@
     def transform(z):
         return jnp.dot(ahead_v[...], jnp.concatenate([z, z], axis=0), preferred_element_type=F32)
 
-    def analyse(whole, rx, sig, rig=None):
+    def analyse(whole, rx, sig, rig=None, step=None):
         whole().wait_recv()
         z = [jnp.concatenate(turn(*[rx[4 * p + n] for n in range(4)], masks_q), axis=0) for p in range(tiles)]
-        for p in range(0, tiles, 2):
-            spec = transform(jnp.concatenate(z[p : p + 2], axis=1))
-            for k in range(2):
-                half = spec[:, k * LANES : (k + 1) * LANES]
-                sig[p + k] = half
-                if rig is not None:
-                    rig[p + k] = pltpu.roll(half, LANES // 2, 1)
-
-    def swap_grads():
-        for p in range(tiles):
-            rigg[p] = pltpu.roll(sigg[p], LANES // 2, 1)
-
-    low, _ = groups(8, F32)
+        if step is None:
+            for p in range(0, tiles, 2):
+                spec = transform(jnp.concatenate(z[p : p + 2], axis=1))
+                sig[p] = spec[:, 0:LANES]
+                sig[p + 1] = spec[:, LANES:]
+            return
+        low_w, _ = masks_w
+        blank = jnp.zeros(z[0].shape, BF16)
+        swapped = [blank] + [pltpu.roll(tile, LANES // 2, 1) for tile in z] + [blank]
+        for p in range(tiles):
+            shifted = jnp.where(low_w, swapped[p + step], swapped[p + step + 1])
+            spec = transform(jnp.concatenate([z[p], shifted], axis=1))
+            sig[p] = spec[:, 0:LANES]
+            rig[p] = spec[:, LANES:]
+
+    def shift_grads():
+        low_f, _ = groups(2 * length, F32)
+        for p in range(tiles):
+            ahead_of = sigg[p + 1] if p + 1 < tiles else jnp.zeros((2 * length, LANES), F32)
+            rigg[p] = pltpu.roll(jnp.where(low_f, ahead_of, sigg[p]), LANES // 2, 1)
+
     parity = lax.rem(lax.broadcasted_iota(jnp.int32, (8, LANES), 0), 2)
     alt = jnp.where(parity == 0, 1.0, -1.0).astype(F32)
     zero = jnp.zeros((8, LANES), F32)
 
-    def windows(re, im):
-        x_re = [zero] + [sigx[p, re, :] for p in range(tiles)]
-        x_im = [zero] + [sigx[p, im, :] for p in range(tiles)]
-        r_re = [zero] + [rigx[p, re, :] for p in range(tiles)]
-        r_im = [zero] + [rigx[p, im, :] for p in range(tiles)]
+    def windows(re, im, count=tiles):
+        x_re = [zero] + [sigx[p, re, :] for p in range(count)]
+        x_im = [zero] + [sigx[p, im, :] for p in range(count)]
         z_re, z_im = [[], []], [[], []]
-        for p in range(tiles):
-            before_re, before_im = jnp.where(low, r_re[p], r_re[p + 1]), jnp.where(low, r_im[p], r_im[p + 1])
+        for p in range(count):
+            before_re, before_im = rigx[p, re, :], rigx[p, im, :]
             z_re[0].append(x_re[p + 1] - alt * before_im)
             z_im[0].append(x_im[p + 1] + alt * before_re)
             z_re[1].append(before_re - alt * x_im[p] if p else before_re)
@@ -308,58 +314,59 @@
     def rows_at(i, start):
         return pl.ds(pl.multiple_of(start + i * 8, 8), 8)
 
-    def correlate():
+    def correlate(n):
         @pl.loop(0, length // 8, unroll=2)
         def _(i):
             re, im = rows_at(i, 0), rows_at(i, length)
-            z_re, z_im = windows(re, im)
-            g_re = [sigg[p, re, :] for p in range(tiles)]
-            g_im = [sigg[p, im, :] for p in range(tiles)]
-            for j in range(nctx):
+            z_re, z_im = windows(re, im, tiles - 2 * n)
+            g_re = {p: sigg[p, re, :] for p in range(2 * n, tiles)}
+            g_im = {p: sigg[p, im, :] for p in range(2 * n, tiles)}
+            for j in range(4 * n, 4 * n + 4):
                 b_re, b_im = z_re[j % 2], z_im[j % 2]
                 ms = [(m, m - j // 2) for m in range(j // 2, tiles)]
                 acc[j, re, :] = total(g_re[m] * b_re[k] + g_im[m] * b_im[k] for m, k in ms)
                 acc[j, im, :] = total(g_im[m] * b_re[k] - g_re[m] * b_im[k] for m, k in ms)
 
         low_f, even_f = groups(64, F32)
-
-        def swing(here, there):
-            return pltpu.roll(jnp.where(low_f, here, there), LANES // 2, 1)
-
-        chunks = [(n, slice(m, m + 64)) for m in range(0, 2 * length, 64) for n in range(nctx // 4)]
-        for n, rows in chunks:
+        chunks = [slice(m, m + 64) for m in range(0, 2 * length, 64)]
+        for rows in chunks:
             for k in (0, 2):
                 a, b = acc[4 * n + k, rows, :], acc[4 * n + k + 1, rows, :]
                 moved = pltpu.roll(jnp.where(even_f, b, a), LANES // 4, 1)
                 acc[4 * n + k, rows, :] = jnp.where(even_f, a, b) + moved
-        for n, rows in chunks:
+        for rows in chunks:
             a, b = acc[4 * n, rows, :], acc[4 * n + 2, rows, :]
-            gfs[rows, n * LANES : (n + 1) * LANES] = (jnp.where(low_f, a, b) + swing(b, a)).astype(BF16)
-
-    def inverse(high):
-        return jnp.dot(back_v[...], jnp.concatenate([high, high], axis=0), preferred_element_type=F32).astype(BF16)
-
-    def send_taps(dp, rsem, here=False):
-        for c in others:
-            copy_g2(c, dp, rsem).start()
-        if not here:
-            copy_g2(me, dp, rsem).start()
-
-    def send_pair(index):
+            moved = pltpu.roll(jnp.where(low_f, b, a), LANES // 2, 1)
+            gfs[n, rows, :] = (jnp.where(low_f, a, b) + moved).astype(BF16)
+
+    def inverse(spec):
+        return jnp.dot(back_v[...], spec, preferred_element_type=F32).astype(BF16)
+
+    def send_taps(dp, rsem, sets=range(nctx // 4)):
+        for n in sets:
+            for c in range(4 * n, 4 * n + 4):
+                copy_g2(c, dp, rsem).start()
+
+    def send_here(rsem, sets=range(nctx // 4)):
+        for n in sets:
+            for c in range(4 * n, 4 * n + 4):
+
+                @pl.when(me != c)
+                def _():
+                    copy_g2(c, row, rsem).start()
+
+    def send_pair(index, sets=range(nctx // 4)):
         @pl.when(part == index)
         def _():
-            send_taps(row, g2_rsem, True)
+            send_here(g2_rsem, sets)
 
         @pl.when(part != index)
         def _():
-            send_taps(other, g2_rsem)
-
-    def finish_taps():
-        taps = inverse(gfs[...])
-        for n in range(nctx // 4):
-            for m, piece in enumerate(turn_rows(taps[:, n * LANES : (n + 1) * LANES], masks_q)):
-                g2_send[4 * n + m] = piece
-        g2_rx[slot] = g2_send[me]
+            send_taps(other, g2_rsem, sets)
+
+    def finish_taps(n):
+        for m, piece in enumerate(turn_rows(inverse(gfs[n]), masks_q)):
+            g2_send[4 * n + m] = piece
 
     def weigh():
         all_f().wait_recv()
@@ -402,11 +409,9 @@
         w_re, w_im = weights(re, im)
         g_re = [sigg[p, re, :] for p in range(tiles)]
         g_im = [sigg[p, im, :] for p in range(tiles)]
-        r_re = [rigg[p, re, :] for p in range(tiles)] + [zero]
-        r_im = [rigg[p, im, :] for p in range(tiles)] + [zero]
         z_re, z_im = [[], []], [[], []]
         for p in range(tiles):
-            after_re, after_im = jnp.where(low, r_re[p], r_re[p + 1]), jnp.where(low, r_im[p], r_im[p + 1])
+            after_re, after_im = rigg[p, re, :], rigg[p, im, :]
             z_re[0].append(g_re[p] + alt * after_im)
             z_im[0].append(g_im[p] - alt * after_re)
             z_re[1].append(after_re + alt * g_im[p + 1] if p + 1 < tiles else after_re)
@@ -434,38 +439,45 @@
         spread_taps()
         spread_grads()
         greet()
-        analyse(all_x, rxx, sigx, rigx)
+        analyse(all_x, rxx, sigx, rigx, 0)
         weigh()
         over_rows(othx, mix_x)
         give_back(othx, mx_send, mx_rx, copy_mx)
-        analyse(all_g, rxg, sigg, rigg)
+        analyse(all_g, rxg, sigg, rigg, 1)
+        correlate(0)
+        finish_taps(0)
+        send_pair(0, [0])
         over_rows(othg, mix_g)
         give_back(othg, mg_send, mg_rx, copy_mg)
-        correlate()
-        finish_taps()
-        send_pair(0)
+        for n in range(1, nctx // 4):
+            correlate(n)
+            finish_taps(n)
+            send_pair(0, [n])
         for dp in range(ndp // 2, ndp):
             send_taps(dp, g2_rsem)
         send_pair(1)
+        g2_rx[slot] = g2_send[me]
 
     @pl.when(jnp.logical_not(early))
     def _():
         spread_grads()
         spread_taps()
         greet()
-        analyse(all_x, rxx, sigx, rigx)
+        analyse(all_x, rxx, sigx, rigx, 0)
         analyse(all_g, rxg, sigg)
-        correlate()
-        finish_taps()
-        for dp in range(ndp // 2):
-            send_taps(dp, g2_rsem)
-        send_taps(row, own_rsem, True)
+        for n in range(nctx // 4):
+            correlate(n)
+            finish_taps(n)
+            for dp in range(ndp // 2):
+                send_taps(dp, g2_rsem, [n])
+        send_here(own_rsem)
         weigh()
-        swap_grads()
+        shift_grads()
         over_rows(othx, mix_x)
         give_back(othx, mx_send, mx_rx, copy_mx)
         over_rows(othg, mix_g)
         give_back(othg, mg_send, mg_rx, copy_mg)
+        g2_rx[slot] = g2_send[me]
         wait_g2(own_rsem, nctx - 1).wait_recv()
         forward(row).start()
 
@@ -558,7 +570,7 @@
             pltpu.VMEM((tiles, 2 * length, LANES), BF16),
             pltpu.VMEM((tiles, 2 * length, LANES), BF16),
             pltpu.VMEM((nctx, 2 * length, LANES), F32),
-            pltpu.VMEM((2 * length, nctx // 4 * LANES), BF16),
+            pltpu.VMEM((nctx // 4, 2 * length, LANES), BF16),
             pltpu.VMEM((nctx, ql, LANES), BF16),
             pieces,
             pieces,

time: 22.7 us -> 22.2 us (0.978)
  the two profiles are of different devices: /device:TPU:0 before, /device:TPU:9 now
where the time goes in v3:
time: 22.2 us; the launch traced here: 22.1 us
  Pallas kernels  21.4 us (96%)
  between operations  0.64 us (3%)
    pallas_call x1, Pallas kernels, fused(): pl.pallas_call(functools.partial(kernel, nctx, ndp), out_shape=(pltpu.VME...  20.5 us
    pallas_call x1, Pallas kernels, fused(): pl.pallas_call(finish, out_shape=(wide, wide, wide, wide, jax.ShapeDtypeS...  0.91 us

profile of v3, /device:TPU:9, one launch (start us, length us, event | category | flops | bytes accessed | tf_op | source)
XLA Modules:
  0.0 22.1 jit_solution(6339727676285422968)
XLA Ops:
  0.6 20.5 %shard_map.110 = (bf16[32,32,128]{2,1,0:T(8,128)(2,1)S(1)}, bf16[1,128,512]{2,1,0:T(8,128)(2,1)S(1)}, bf16[1,128,512]{2,1,0:T(8,128)(2,1)S(1)}, bf16[1,128,512]{2,1,0:T(8,128)(2,1)S(1)}, bf16[1,128,512]{2,1,0:T(8,128)(2,1)S(1)}) custom-call(bf16[1,128,512]{2,1,0:T(8,128)(2,1)} %q_hbm.1, bf16[1,128,512]{2,1,0:T(8,128)(2,1)} %k_hbm.1, ...), custom_call_target="tpu_custom_call" | custom-call | tf_op jit(solution)/shard_map/pallas_call | solution.py:544
  21.2 0.9 %shard_map.111 = (bf16[1,128,512]{2,1,0:T(8,128)(2,1)}, bf16[1,128,512]{2,1,0:T(8,128)(2,1)}, bf16[1,128,512]{2,1,0:T(8,128)(2,1)}, bf16[1,128,512]{2,1,0:T(8,128)(2,1)}, f32[128,512]{1,0:T(8,128)}) custom-call(bf16[32,32,128]{2,1,0:T(8,128)(2,1)S(1)} %get-tuple-element.10.g2, bf16[1,128,512]{2,1,0:T(8,128)(2,1)S(1)} %get-tuple-element.11.out, ...), custom_call_target="tpu_custom_call" | custom-call | tf_op jit(solution)/shard_map/pallas_call | solution.py:586

commit v4 on v3

--- a/solution.py
+++ b/solution.py
@@ -449,13 +449,15 @@
         send_pair(0, [0])
         over_rows(othg, mix_g)
         give_back(othg, mg_send, mg_rx, copy_mg)
-        for n in range(1, nctx // 4):
-            correlate(n)
-            finish_taps(n)
-            send_pair(0, [n])
-        for dp in range(ndp // 2, ndp):
-            send_taps(dp, g2_rsem)
-        send_pair(1)
+        for n in range(nctx // 4):
+            if n:
+                correlate(n)
+                finish_taps(n)
+            for dp in reversed(range(ndp // 2, ndp)):
+                send_taps(dp, g2_rsem, [n])
+            if n:
+                send_pair(0, [n])
+            send_pair(1, [n])
         g2_rx[slot] = g2_send[me]
 
     @pl.when(jnp.logical_not(early))

time: 22.2 us -> 21.8 us (0.982)
  the two profiles are of different devices: /device:TPU:9 before, /device:TPU:13 now
where the time goes in v4:
time: 21.8 us; the launch traced here: 21.7 us
  Pallas kernels  21 us (96%)
  between operations  0.64 us (3%)
    pallas_call x1, Pallas kernels, fused(): pl.pallas_call(functools.partial(kernel, nctx, ndp), out_shape=(pltpu.VME...  20.1 us
    pallas_call x1, Pallas kernels, fused(): pl.pallas_call(finish, out_shape=(wide, wide, wide, wide, jax.ShapeDtypeS...  0.91 us

profile of v4, /device:TPU:13, one launch (start us, length us, event | category | flops | bytes accessed | tf_op | source)
XLA Modules:
  0.0 21.7 jit_solution(14755044706118545600)
XLA Ops:
  0.6 20.1 %shard_map.110 = (bf16[32,32,128]{2,1,0:T(8,128)(2,1)S(1)}, bf16[1,128,512]{2,1,0:T(8,128)(2,1)S(1)}, bf16[1,128,512]{2,1,0:T(8,128)(2,1)S(1)}, bf16[1,128,512]{2,1,0:T(8,128)(2,1)S(1)}, bf16[1,128,512]{2,1,0:T(8,128)(2,1)S(1)}) custom-call(bf16[1,128,512]{2,1,0:T(8,128)(2,1)} %q_hbm.1, bf16[1,128,512]{2,1,0:T(8,128)(2,1)} %k_hbm.1, ...), custom_call_target="tpu_custom_call" | custom-call | tf_op jit(solution)/shard_map/pallas_call | solution.py:546
  20.8 0.9 %shard_map.111 = (bf16[1,128,512]{2,1,0:T(8,128)(2,1)}, bf16[1,128,512]{2,1,0:T(8,128)(2,1)}, bf16[1,128,512]{2,1,0:T(8,128)(2,1)}, bf16[1,128,512]{2,1,0:T(8,128)(2,1)}, f32[128,512]{1,0:T(8,128)}) custom-call(bf16[32,32,128]{2,1,0:T(8,128)(2,1)S(1)} %get-tuple-element.10.g2, bf16[1,128,512]{2,1,0:T(8,128)(2,1)S(1)} %get-tuple-element.11.out, ...), custom_call_target="tpu_custom_call" | custom-call | tf_op jit(solution)/shard_map/pallas_call | solution.py:588

commit v5 on v4

--- a/solution.py
+++ b/solution.py
@@ -474,9 +474,9 @@
                 send_taps(dp, g2_rsem, [n])
         send_here(own_rsem)
         weigh()
-        shift_grads()
         over_rows(othx, mix_x)
         give_back(othx, mx_send, mx_rx, copy_mx)
+        shift_grads()
         over_rows(othg, mix_g)
         give_back(othg, mg_send, mg_rx, copy_mg)
         g2_rx[slot] = g2_send[me]

time: 21.8 us -> 21.8 us (level)
  no operation moved by 1% of the time
where the time goes in v5:
time: 21.8 us; the launch traced here: 21.7 us
  Pallas kernels  21 us (96%)
  between operations  0.64 us (3%)
    pallas_call x1, Pallas kernels, fused(): pl.pallas_call(functools.partial(kernel, nctx, ndp), out_shape=(pltpu.VME...  20.1 us
    pallas_call x1, Pallas kernels, fused(): pl.pallas_call(finish, out_shape=(wide, wide, wide, wide, jax.ShapeDtypeS...  0.91 us

profile of v5, /device:TPU:13, one launch (start us, length us, event | category | flops | bytes accessed | tf_op | source)
XLA Modules:
  0.0 21.7 jit_solution(17559022953224028493)
XLA Ops:
  0.6 20.1 %shard_map.110 = (bf16[32,32,128]{2,1,0:T(8,128)(2,1)S(1)}, bf16[1,128,512]{2,1,0:T(8,128)(2,1)S(1)}, bf16[1,128,512]{2,1,0:T(8,128)(2,1)S(1)}, bf16[1,128,512]{2,1,0:T(8,128)(2,1)S(1)}, bf16[1,128,512]{2,1,0:T(8,128)(2,1)S(1)}) custom-call(bf16[1,128,512]{2,1,0:T(8,128)(2,1)} %q_hbm.1, bf16[1,128,512]{2,1,0:T(8,128)(2,1)} %k_hbm.1, ...), custom_call_target="tpu_custom_call" | custom-call | tf_op jit(solution)/shard_map/pallas_call | solution.py:546
  20.8 0.9 %shard_map.111 = (bf16[1,128,512]{2,1,0:T(8,128)(2,1)}, bf16[1,128,512]{2,1,0:T(8,128)(2,1)}, bf16[1,128,512]{2,1,0:T(8,128)(2,1)}, bf16[1,128,512]{2,1,0:T(8,128)(2,1)}, f32[128,512]{1,0:T(8,128)}) custom-call(bf16[32,32,128]{2,1,0:T(8,128)(2,1)S(1)} %get-tuple-element.10.g2, bf16[1,128,512]{2,1,0:T(8,128)(2,1)S(1)} %get-tuple-element.11.out, ...), custom_call_target="tpu_custom_call" | custom-call | tf_op jit(solution)/shard_map/pallas_call | solution.py:588
